TPU v7x, 512 devices: a whole 4x4x16 slice. The times are simulated.
512 devices in a mesh: dp: 128 (over z, x, core), mp: 4 (over y).
Axes of the slice: x: 4, y: 4, z: 16, core: 2. Of those that a mesh axis runs over, the one named last changes fastest.
Arguments:
- grad_blocks: bfloat16 [256, 128, 128], P('dp', None, 'mp'), may hold values from -0.5 to 0.5
- owner_table: int32 [256], replicated, may hold values from 0 to 127, as said below
- prev_stats: float32 [1024, 2, 128, 128], P('dp'), as said below
Outputs:
- update: bfloat16 [256, 128, 128], P('dp', None, 'mp')
- new_stats: float32 [1024, 2, 128, 128], P('dp')
- inv_roots: float32 [1024, 2, 128, 128], P('dp')
Inputs may be any that keep to these rules, and one draw needn't show every extreme that they name: `owner_table`: every entry is a dp index; no index appears more than 8 times, and some index appears exactly 8 times. `prev_stats`: each [128, 128] matrix is symmetric positive semidefinite.
All inputs are finite; a program needn't handle non-finite values.
Results may differ from a plain program's by a relative error of at most 0.001.
Values may be sent and summed in bfloat16 or wider, within the bound.
A program may use at most 64 MiB of HBM per device.

v0:
```python
import jax
import jax.numpy as jnp
from jax import lax
from jax.sharding import PartitionSpec as P

ITERS = 16


STAT_DECAY = 0.75
DAMPING = 0.03


def batch_product(first, second):
    return jnp.einsum("pij,pjk->pik", first, second, precision=lax.Precision.HIGHEST)


def newton_roots(matrices):
    width = matrices.shape[-1]
    identity = jnp.eye(width, dtype=jnp.float32)
    trace_val = jnp.trace(matrices, axis1=1, axis2=2)
    damped = matrices + DAMPING / width * trace_val[:, None, None] * identity
    norm_val = jnp.sqrt(jnp.sum(damped * damped, axis=(1, 2)))
    root_mat = identity * (1.0 / jnp.sqrt(jnp.sqrt(norm_val)))[:, None, None]
    remainder = damped / norm_val[:, None, None]

    def refine(unused, state_pair):
        root_now, rest_now = state_pair
        factor = (5.0 * identity - rest_now) * 0.25
        root_now = batch_product(root_now, factor)
        square = batch_product(factor, factor)
        quartic = batch_product(square, square)
        return (root_now, batch_product(quartic, rest_now))

    root_mat, remainder = lax.fori_loop(0, ITERS, refine, (root_mat, remainder))
    return root_mat


def per_device(grad_blocks, owner_table, prev_stats):
    dev_count = lax.axis_size("dp")
    my_index = lax.axis_index("dp")
    part_count = lax.axis_size("mp")
    part_index = lax.axis_index("mp")
    blk_local = grad_blocks.shape[0]
    width = grad_blocks.shape[1]
    part_width = grad_blocks.shape[2]
    capacity = prev_stats.shape[0]
    block_total = owner_table.shape[0]
    home_owner = lax.dynamic_slice_in_dim(owner_table, my_index * blk_local, blk_local)
    send_mask = jnp.arange(dev_count, dtype=jnp.int32)[:, None] == home_owner[None, :]
    owned_mask = (owner_table == my_index).astype(jnp.int32)
    slot_rank = jnp.cumsum(owned_mask) - owned_mask
    slot_range = jnp.arange(capacity, dtype=jnp.int32)
    picker = ((owned_mask[None, :] == 1) & (slot_rank[None, :] == slot_range[:, None])).astype(
        jnp.bfloat16
    )
    filled = slot_range < jnp.sum(owned_mask)

    def route(blocks):
        return jnp.where(send_mask[:, :, None, None], blocks[None], jnp.zeros((), blocks.dtype))

    def pick(arrived):
        flat = arrived.reshape(block_total, -1)
        chosen = jnp.dot(picker, flat, preferred_element_type=jnp.float32)
        return chosen.astype(jnp.bfloat16).reshape((capacity,) + arrived.shape[2:])

    arrived = lax.all_to_all(route(grad_blocks), "dp", split_axis=0, concat_axis=0, tiled=True)
    whole = lax.all_gather(pick(arrived), "mp", axis=2, tiled=True)
    left_stat = jnp.einsum("rik,rjk->rij", whole, whole, preferred_element_type=jnp.float32)
    right_stat = jnp.einsum("rki,rkj->rij", whole, whole, preferred_element_type=jnp.float32)
    blended = STAT_DECAY * prev_stats + (1.0 - STAT_DECAY) * jnp.stack(
        [left_stat, right_stat], axis=1
    )
    new_stats = jnp.where(filled[:, None, None, None], blended, 0.0)
    identity = jnp.eye(width, dtype=jnp.float32)
    problems = jnp.where(filled[:, None, None, None], blended, identity).reshape(
        2 * capacity, width, width
    )
    share = 2 * capacity // part_count
    my_problems = lax.dynamic_slice_in_dim(problems, part_index * share, share, 0)
    roots_flat = lax.all_gather(newton_roots(my_problems), "mp", axis=0, tiled=True)
    roots = roots_flat.reshape(capacity, 2, width, width)
    inv_roots = jnp.where(filled[:, None, None, None], roots, 0.0)
    whole_wide = whole.astype(jnp.float32)
    precond = jnp.einsum("rij,rjk->rik", roots[:, 0], whole_wide, precision=lax.Precision.HIGHEST)
    precond = jnp.einsum("rij,rjk->rik", precond, roots[:, 1], precision=lax.Precision.HIGHEST)
    spread = jnp.sqrt(jnp.mean(precond * precond, axis=(1, 2)))
    spread = jnp.where(filled, spread, 1.0)
    scaled = (precond / spread[:, None, None]).astype(jnp.bfloat16)
    columns = lax.dynamic_slice_in_dim(scaled, part_index * part_width, part_width, 2)
    outgoing = jnp.dot(picker.T, columns.reshape(capacity, -1), preferred_element_type=jnp.float32)
    outgoing = outgoing.astype(jnp.bfloat16).reshape(dev_count, blk_local, width, part_width)
    returned = lax.all_to_all(outgoing, "dp", split_axis=0, concat_axis=0, tiled=True)
    update = returned[home_owner, jnp.arange(blk_local, dtype=jnp.int32)]
    return (update, new_stats, inv_roots)


def solution(mesh):
    return jax.shard_map(
        per_device,
        mesh=mesh,
        in_specs=(P("dp", None, "mp"), P(), P("dp", None, None, None)),
        out_specs=(P("dp", None, "mp"), P("dp", None, None, None), P("dp", None, None, None)),
        check_vma=False,
    )
```

profile of v0, /device:TPU:1, one launch (start us, length us, event | category | flops | bytes accessed | tf_op | source)
XLA Modules:
  0.0 364.0 jit_solution(6509518457858769847)
XLA Ops:
  7.2 0.8 fusion.27
  7.9 2.3 broadcast_select_fusion
  10.2 20.5 %all-to-all-start = ((bf16[128,2,128,32]{2,3,1,0:T(8,128)(2,1)}), bf16[128,2,128,32]{2,3,1,0:T(8,128)(2,1)S(1)}, u32[]{:S(2)}, u32[]{:S(2)}) async-start(bf16[128,2,128,32]{2,3,1,0:T(8,128)(2,1)} %broadcast_select_fusion), calls=%async_computation | async-start | bytes 4194304 | tf_op jit(solution)/shard_map/all_to_all | solution.py:66
  31.4 0.6 fusion.28
  32.0 0.6 iota_compare_fusion.4
  32.7 97.1 %all-to-all-done = bf16[128,2,128,32]{2,3,1,0:T(8,128)(2,1)S(1)} async-done(((bf16[128,2,128,32]{2,3,1,0:T(8,128)(2,1)}), bf16[128,2,128,32]{2,3,1,0:T(8,128)(2,1)S(1)}, u32[]{:S(2)}, u32[]{:S(2)}) %all-to-all-start) | async-done | bytes 2097184 | tf_op jit(solution)/shard_map/all_to_all | solution.py:66
  129.8 6.5 %copy.32 = bf16[128,2,128,32]{3,2,1,0:T(8,128)(2,1)} copy(bf16[128,2,128,32]{2,3,1,0:T(8,128)(2,1)S(1)} %all-to-all-done) | data formatting | bytes 4194304 | tf_op jit(solution)/shard_map/all_to_all | solution.py:66
  136.2 10.7 %reshape.97 = bf16[256,4096]{1,0:T(8,128)(2,1)S(1)} reshape(bf16[128,2,128,32]{3,2,1,0:T(8,128)(2,1)} %copy.32) | data formatting | bytes 4194304 | tf_op jit(solution)/shard_map/reshape | solution.py:62
  146.9 0.4 convolution_convert_fusion.1
  147.6 9.9 %all_gather.6 = bf16[8,128,128]{1,2,0:T(8,128)(2,1)S(1)} all-gather(bf16[8,128,32]{1,2,0:T(8,128)(2,1)S(1)} %copy.33), channel_id=1, replica_groups=mesh['dp'=128,'mp'=4] {'mp'}, dimensions={2}, use_global_device_ids=true | all-gather | bytes 327680 | tf_op jit(solution)/shard_map/all_gather | solution.py:67
  159.1 29.6 %while.13 = (s32[]{:T(128)}, f32[4,128,128]{1,2,0:T(8,128)S(1)}, f32[4,128,128]{2,1,0:T(8,128)S(1)}, s32[]{:T(128)}) while((s32[]{:T(128)}, f32[4,128,128]{1,2,0:T(8,128)S(1)}, f32[4,128,128]{2,1,0:T(8,128)S(1)}, s32[]{:T(128)}) %tuple.39), condition=%wide.region_6.7_spmd.clone, body=%wide.region_5.6_spmd.clone.sunk | while | flops 402948096 | bytes 3866677 | solution.py:34
  159.2 0.4 fusion.62
  160.0 0.6 convolution_bitcast_fusion.4
  160.6 0.4 fusion.64
  161.1 0.4 fusion.62
  161.8 0.6 convolution_bitcast_fusion.4
  162.4 0.4 fusion.64
  162.9 0.4 fusion.62
  163.7 0.6 convolution_bitcast_fusion.4
  164.3 0.4 fusion.64
  164.8 0.4 fusion.62
  165.5 0.6 convolution_bitcast_fusion.4
  166.1 0.4 fusion.64
  167.4 0.6 convolution_bitcast_fusion.4
  168.0 0.4 fusion.64
  169.2 0.6 convolution_bitcast_fusion.4
  169.8 0.4 fusion.64
  171.1 0.6 convolution_bitcast_fusion.4
  171.7 0.4 fusion.64
  172.9 0.6 convolution_bitcast_fusion.4
  173.5 0.4 fusion.64
  174.0 0.4 fusion.62
  174.7 0.6 convolution_bitcast_fusion.4
  175.4 0.4 fusion.64
  176.6 0.6 convolution_bitcast_fusion.4
  177.2 0.4 fusion.64
  178.4 0.6 convolution_bitcast_fusion.4
  179.1 0.4 fusion.64
  180.3 0.6 convolution_bitcast_fusion.4
  180.9 0.4 fusion.64
  181.4 0.4 fusion.62
  182.1 0.6 convolution_bitcast_fusion.4
  182.7 0.4 fusion.64
  184.0 0.6 convolution_bitcast_fusion.4
  184.6 0.4 fusion.64
  185.8 0.6 convolution_bitcast_fusion.4
  186.4 0.4 fusion.64
  187.7 0.6 convolution_bitcast_fusion.4
  188.3 0.4 fusion.64
  188.7 0.8 copy.36
  189.6 26.4 %all-gather.2.cloned.1.call-done = f32[16,128,128]{2,1,0:T(8,128)} async-done(((f32[4,128,128]{2,1,0:T(8,128)}), f32[16,128,128]{2,1,0:T(8,128)}) %all-gather.2.cloned.1.call-update) | async-done | bytes 1048592 | tf_op jit(solution)/shard_map/all_gather | solution.py:80
  216.0 2.5 broadcast_select_fusion.1
  218.4 0.7 fusion.12
  219.1 1.1 multiply_reduce_fusion
  220.2 0.7 sqrt_select_fusion
  221.4 0.8 convolution_convert_fusion
  222.2 8.0 %reshape.102 = bf16[128,2,128,32]{3,2,1,0:T(8,128)(2,1)} reshape(bf16[256,4096]{1,0:T(8,128)(2,1)S(1)} %convolution_convert_fusion) | data formatting | bytes 4194304 | tf_op jit(solution)/shard_map/reshape | solution.py:91
  230.2 7.9 %copy.40 = bf16[128,2,128,32]{2,3,1,0:T(8,128)(2,1)} copy(bf16[128,2,128,32]{3,2,1,0:T(8,128)(2,1)} %reshape.102) | data formatting | bytes 4194304 | tf_op jit(solution)/shard_map/reshape | solution.py:91
  238.1 18.8 %all-to-all-start.1 = ((bf16[128,2,128,32]{2,3,1,0:T(8,128)(2,1)}), bf16[128,2,128,32]{2,3,1,0:T(8,128)(2,1)S(1)}, u32[]{:S(2)}, u32[]{:S(2)}) async-start(bf16[128,2,128,32]{2,3,1,0:T(8,128)(2,1)} %copy.40), calls=%async_computation.1 | async-start | bytes 4194304 | tf_op jit(solution)/shard_map/all_to_all | solution.py:92
  257.0 1.0 copy.42
  258.0 0.6 copy-done
  258.6 1.1 copy.43
  259.6 96.3 %all-to-all-done.1 = bf16[128,2,128,32]{2,3,1,0:T(8,128)(2,1)S(1)} async-done(((bf16[128,2,128,32]{2,3,1,0:T(8,128)(2,1)}), bf16[128,2,128,32]{2,3,1,0:T(8,128)(2,1)S(1)}, u32[]{:S(2)}, u32[]{:S(2)}) %all-to-all-start.1) | async-done | bytes 2097184 | tf_op jit(solution)/shard_map/all_to_all | solution.py:92
  356.0 1.2 gather_fusion
  (106 shorter events, 13.3 us)
Async XLA Ops:
  10.2 20.6 %copy-start.3 = (s32[256]{0:T(256)S(1)}, s32[256]{0:T(256)}, u32[]{:S(2)}) copy-start(s32[256]{0:T(256)} %param.6) | copy-start | bytes 3076
  10.2 119.5 %all-to-all-start = ((bf16[128,2,128,32]{2,3,1,0:T(8,128)(2,1)}), bf16[128,2,128,32]{2,3,1,0:T(8,128)(2,1)S(1)}, u32[]{:S(2)}, u32[]{:S(2)}) async-start(bf16[128,2,128,32]{2,3,1,0:T(8,128)(2,1)} %broadcast_select_fusion), calls=%async_computation | async-start | bytes 4194304 | tf_op jit(solution)/shard_map/all_to_all | solution.py:66
  30.8 185.2 %all-gather.2.cloned.1.call-start = ((), (), s32[]{:S(2)}) async-start(), calls=%async_computation.2 | async-start | bytes 1310720 | tf_op jit(solution)/shard_map/all_gather | solution.py:80
  146.9 11.2 %copy-start.2 = (f32[8,2,128,128]{3,2,1,0:T(8,128)S(1)}, f32[8,2,128,128]{3,2,1,0:T(8,128)}, u32[]{:S(2)}) copy-start(f32[8,2,128,128]{3,2,1,0:T(8,128)} %param.7) | copy-start | bytes 3145732
  216.0 3.1 copy-start.1
  238.1 117.9 %all-to-all-start.1 = ((bf16[128,2,128,32]{2,3,1,0:T(8,128)(2,1)}), bf16[128,2,128,32]{2,3,1,0:T(8,128)(2,1)S(1)}, u32[]{:S(2)}, u32[]{:S(2)}) async-start(bf16[128,2,128,32]{2,3,1,0:T(8,128)(2,1)} %copy.40), calls=%async_computation.1 | async-start | bytes 4194304 | tf_op jit(solution)/shard_map/all_to_all | solution.py:92
  257.0 1.6 copy-start
Sparse Core Ops, SparseCore 0:
  189.7 26.2 all-gather.1
where the time goes:
time: 366 us; the launch traced here: 364 us
  waiting for transfers between devices  220 us (60%)
  local copies, waits for them, and re-layouts  39.5 us (11%)
  starting transfers between devices  39.4 us (11%)
  matrix products  31.2 us (9%)
  between operations  14.2 us (4%)
  blocking collectives  9.89 us (3%)
  other arithmetic  8.89 us (2%)
    all_to_all x1, waiting for transfers between devices, per_device(): lax.all_to_all(route(grad_blocks), 'dp', split_axis=0, concat_axis=0, til...  97.1 us
    all_to_all x1, waiting for transfers between devices, per_device(): lax.all_to_all(outgoing, 'dp', split_axis=0, concat_axis=0, tiled=True)  96.3 us
    dot_general x64, matrix products, batch_product(): jnp.einsum('pij,pjk->pik', first, second, precision=lax.Precision.HIGHEST)  27.7 us
    all_gather x1, waiting for transfers between devices, per_device(): lax.all_gather(newton_roots(my_problems), 'mp', axis=0, tiled=True)  26.4 us
    all_to_all x1, starting transfers between devices, per_device(): lax.all_to_all(route(grad_blocks), 'dp', split_axis=0, concat_axis=0, til...  20.5 us
    all_to_all x1, starting transfers between devices, per_device(): lax.all_to_all(outgoing, 'dp', split_axis=0, concat_axis=0, tiled=True)  18.8 us
    reshape x2, local copies, waits for them, and re-layouts, per_device(): outgoing.astype(jnp.bfloat16)  15.9 us
    reshape x1, local copies, waits for them, and re-layouts, pick(): flat = arrived.reshape(block_total, -1)  10.7 us
  transfers between devices with their start and end apart: 3, of which 3 were waited for; matrix products, arithmetic and copies ran while one was open for 1% of the time, Pallas kernels for 0%

commit v1 on v0

v1 whole, which is shorter than its diff:
```python
import jax
import jax.numpy as jnp
from jax import lax
from jax.experimental import pallas as pl
from jax.experimental.pallas import tpu as pltpu
from jax.sharding import PartitionSpec as P

ITERS = 16
STAT_DECAY = 0.75
DAMPING = 0.03
N = 128
XS, CORES, YS = 4, 2, 4
CAP = 8
NEAR = 4
MESH = pl.DeviceIdType.MESH
BF = jnp.bfloat16
F32 = jnp.float32


def split(a):
    hi = a.astype(BF)
    return hi, (a - hi.astype(F32)).astype(BF)


def wide(a):
    return jnp.concatenate(split(a), axis=1)


def tall(a):
    row = wide(a)
    return jnp.concatenate([row, row], axis=0)


def product(left, right):
    out = jnp.dot(left, right, preferred_element_type=F32)
    return out[:, :N] + out[:, N:]


def kernel(
    zs,
    grad_ref, owner_ref, prev_ref,
    upd_ref, stats_ref, roots_ref,
    zbuf, sel1, rbuf, gt, prev, stat, root, mstate, xstate, ubuf, vbuf, wbuf, bfar, mfar, abuf, tabv, tabs,
    z_send, z_recv, d_send, d_recv, p_send, p_recv, s_send, s_recv, r_send, r_recv,
    u_send, u_recv, e_send, e_recv, w_send, w_recv, loc,
):
    dp = lax.axis_index("dp")
    q = lax.axis_index("mp")
    z = lax.div(dp, XS * CORES)
    x = lax.rem(lax.div(dp, CORES), XS)
    c = lax.rem(dp, CORES)

    def zoff(d):
        return lax.rem(z + (d + zs), zs)

    def dev(zz, xx, cc, yy):
        return ((zz * XS + xx) * CORES + cc, yy)

    def along(d):
        return dev(zoff(d), x, c, q)

    def plane(dx, dy):
        return lax.rem(x + dx, XS), lax.rem(q + dy, YS)

    other = dev(z, x, 1 - c, q)
    shifts = [(dx, dy) for dx in range(XS) for dy in range(YS) if (dx, dy) != (0, 0)]
    shifts.sort(key=lambda s: -(min(s[0], XS - s[0]) + min(s[1], YS - s[1])))
    steps = [d for k in range(NEAR, 0, -1) for d in (k, -k)]

    def rcopy(src, dst, ssem, rsem, where):
        return pltpu.make_async_remote_copy(
            src_ref=src, dst_ref=dst, send_sem=ssem, recv_sem=rsem,
            device_id=where, device_id_type=MESH)

    barrier = pltpu.get_barrier_semaphore()
    partners = [along(d) for d in steps] + [other]
    for dx, dy in shifts:
        xx, yy = plane(dx, dy)
        partners.append(dev(z, xx, c, yy))
    for where in partners:
        pl.semaphore_signal(barrier, inc=1, device_id=where, device_id_type=MESH)

    my_slots = (x * CORES + c) * CAP + 2 * q
    load_prev = pltpu.make_async_copy(prev_ref.at[pl.ds(2 * q, 2)], prev, loc.at[0])
    load_prev.start()

    owners = owner_ref[...]
    lanes = lax.broadcasted_iota(jnp.int32, (N, N), 1)
    subs = lax.broadcasted_iota(jnp.int32, (N, N), 0)
    rows = [jnp.broadcast_to(owners[h:h + 1, :], (N, N)) for h in range(2)]
    cols = [rows[h].T for h in range(2)]
    want = z * (XS * CORES * CAP) + lanes
    take = jnp.zeros((1, N), jnp.int32)
    filled = jnp.zeros((1, N), jnp.int32)
    n_plane = XS * CORES * CAP
    none_slot = 2 * CORES * zs
    for h in range(2):
        rank_c = jnp.zeros((N, 1), jnp.int32)
        rank_r = jnp.zeros((1, N), jnp.int32)
        for g in range(2):
            before = (cols[h] == rows[g]) & (lanes + N * g < subs + N * h)
            rank_c = rank_c + jnp.sum(before.astype(jnp.int32), axis=1, keepdims=True)
            after = (cols[g] == rows[h]) & (subs + N * g < lanes + N * h)
            rank_r = rank_r + jnp.sum(after.astype(jnp.int32), axis=0, keepdims=True)
        slot_c = cols[h] * CAP + rank_c
        slot_r = owners[h:h + 1, :] * CAP + rank_r
        blk = subs + N * h
        match = (slot_c == want) & (lanes < n_plane)
        place = (((blk >> 1) & 1) * zs + (blk >> 4)) * 2 + (blk & 1)
        here = match & (((blk >> 2) & 3) == x)
        take = take + jnp.sum(jnp.where(here, none_slot - place, 0), axis=0, keepdims=True)
        filled = filled + jnp.sum(match.astype(jnp.int32), axis=0, keepdims=True)
        back = jnp.where(slot_r >> 6 == z, slot_r & (n_plane - 1), n_plane)
        tabv[2 + h:3 + h, :] = back
    tabv[0:1, :] = none_slot - take
    tabv[1:2, :] = filled
    zeros = jnp.zeros((N // YS, N), BF)
    zbuf[none_slot] = zeros
    vbuf[n_plane] = zeros

    pl.semaphore_wait(barrier, len(partners))

    def zplace(cc, zz):
        return (cc * zs + zz) * 2

    sends = []
    zr = {}
    for d in steps:
        cp = rcopy(grad_ref, zbuf.at[pl.ds(zplace(c, z), 2)], z_send.at[len(sends)], z_recv.at[d + 7], along(d))
        cp.start()
        sends.append(cp)
    dcopies = []

    def to_other(src, zz, k):
        cp = rcopy(src, zbuf.at[pl.ds(zplace(c, zz), 2)], d_send.at[k], d_recv.at[k], other)
        cp.start()
        dcopies.append(cp)

    to_other(grad_ref, z, 0)
    tab_copy = pltpu.make_async_copy(tabv, tabs, loc.at[1])
    tab_copy.start()
    zbuf[pl.ds(zplace(c, z), 2)] = grad_ref[...]

    def arrived(d):
        ref = zbuf.at[pl.ds(zplace(c, zoff(-d)), 2)]
        rcopy(ref, ref, z_send.at[0], z_recv.at[d + 7], along(d)).wait_recv()

    for sgn in (1, -1):
        arrived(sgn * NEAR)
        src = zplace(c, zoff(-sgn * NEAR))
        half = zbuf.at[src + (0 if sgn > 0 else 1)]
        cp = rcopy(half, half, z_send.at[len(sends)], z_recv.at[15 if sgn > 0 else 16], along(sgn * NEAR))
        cp.start()
        sends.append(cp)
        whole = zbuf.at[pl.ds(src, 2)]
        for k in range(NEAR - 1, 0, -1):
            cp = rcopy(whole, whole, z_send.at[len(sends)], z_recv.at[sgn * (NEAR + k) + 7], along(sgn * k))
            cp.start()
            sends.append(cp)
    for k, d in enumerate([4, -4, 1, -1, 2, -2, 3, -3, 5, -5, 6, -6, 7, -7]):
        if abs(d) != NEAR:
            arrived(d)
        to_other(zbuf.at[pl.ds(zplace(c, zoff(-d)), 2)], zoff(-d), k + 1)
    for k in range(2):
        ref = zbuf.at[zplace(c, zoff(8)) + k]
        rcopy(ref, ref, z_send.at[0], z_recv.at[15 + k], other).wait_recv()
    to_other(zbuf.at[pl.ds(zplace(c, zoff(8)), 2)], zoff(8), 15)
    order = [0, 4, -4, 1, -1, 2, -2, 3, -3, 5, -5, 6, -6, 7, -7, 8]
    for k, d in enumerate(order):
        ref = zbuf.at[pl.ds(zplace(1 - c, zoff(-d)), 2)]
        rcopy(ref, ref, d_send.at[k], d_recv.at[k], other).wait_recv()

    tab_copy.wait()
    psends = []
    for i, (dx, dy) in enumerate([*shifts, (0, 0)]):
        xx, yy = plane(dx, dy)
        first = (xx * CORES + c) * CAP + 2 * yy
        if (dx, dy) != (0, 0):
            for r in range(2):
                sel1[i, r] = zbuf[tabs[0, first + r]]
            cp = rcopy(sel1.at[i], rbuf.at[x, q], p_send.at[i], p_recv.at[i], dev(z, xx, c, yy))
            cp.start()
            psends.append(cp)
        else:
            for r in range(2):
                rbuf[x, q, r] = zbuf[tabs[0, first + r]]
    for i, (dx, dy) in enumerate(shifts):
        ref = rbuf.at[lax.rem(x + XS - dx, XS), lax.rem(q + YS - dy, YS)]
        rcopy(ref, ref, p_send.at[i], p_recv.at[i], other).wait_recv()
    part = N // YS
    for r in range(2):
        for k in range(YS):
            total = rbuf[0, k, r] + rbuf[1, k, r] + rbuf[2, k, r] + rbuf[3, k, r]
            gt[r, part * k:part * (k + 1), :] = total

    load_prev.wait()
    eye = (lax.broadcasted_iota(jnp.int32, (N, N), 0) == lax.broadcasted_iota(jnp.int32, (N, N), 1)).astype(F32)
    for r in range(2):
        on = tabs[1, my_slots + r].astype(F32)
        g = gt[r]
        sides = [
            lax.dot_general(g, g, (((0,), (0,)), ((), ())), preferred_element_type=F32),
            lax.dot_general(g, g, (((1,), (1,)), ((), ())), preferred_element_type=F32),
        ]
        for k in range(2):
            blended = (STAT_DECAY * prev[r, k] + (1.0 - STAT_DECAY) * sides[k]) * on
            stat[r, k] = blended
            s = blended + (1.0 - on) * eye
            tr = jnp.sum(jnp.sum(s * eye, axis=1, keepdims=True), axis=0, keepdims=True)
            a = s + (DAMPING / N) * tr * eye
            norm = jnp.sqrt(jnp.sum(jnp.sum(a * a, axis=1, keepdims=True), axis=0, keepdims=True))
            xstate[2 * r + k] = eye * (1.0 / jnp.sqrt(jnp.sqrt(norm)))
            mstate[2 * r + k] = a * (1.0 / norm)

    ssends = []

    def share(src, dst_ref, ssem, rsem, lsem):
        mine = dst_ref.at[pl.ds(2 * q, 2)]
        keep = pltpu.make_async_copy(src, mine, lsem)
        keep.start()
        for dy in range(1, YS):
            cp = rcopy(src, mine, ssem.at[dy - 1], rsem.at[dy - 1], dev(z, x, c, lax.rem(q + dy, YS)))
            cp.start()
            ssends.append(cp)
        return keep

    keep_stat = share(stat, stats_ref, s_send, s_recv, loc.at[2])

    def body(it, unused):
        del it, unused
        fs, ms = [], []
        for p in range(4):
            m = mstate[p]
            fs.append(1.25 * eye - 0.25 * m)
            ms.append(wide(m))
        gs = []
        for p in range(4):
            w = wide(fs[p])
            right = jnp.concatenate([w, w], axis=0)
            gs.append(product(w, right))
            xstate[p] = product(wide(xstate[p]), right)
        rights = [tall(g) for g in gs]
        ts = [product(ms[p], rights[p]) for p in range(4)]
        for p in range(4):
            mstate[p] = product(wide(ts[p]), rights[p])
        return 0

    lax.fori_loop(0, ITERS - 1, body, 0)
    for r in range(2):
        on = tabs[1, my_slots + r].astype(F32)
        sides = []
        for k in range(2):
            f = 1.25 * eye - 0.25 * mstate[2 * r + k]
            sides.append(product(wide(xstate[2 * r + k]), tall(f)))
            root[r, k] = sides[k] * on
        g = gt[r]
        t = jnp.dot(wide(sides[1]), jnp.concatenate([g, g], axis=0), preferred_element_type=F32)
        pt = product(wide(t), tall(sides[0]))
        ms = jnp.sum(jnp.sum(pt * pt, axis=1, keepdims=True), axis=0, keepdims=True) * (1.0 / (N * N))
        spread = jnp.sqrt(ms) + (1.0 - on)
        u = (pt / spread).astype(BF)
        for k in range(YS):
            ubuf[k, r] = u[part * k:part * (k + 1), :]

    usends = []
    for i, (dx, dy) in enumerate([(0, 0), *shifts]):
        xx, yy = plane(dx, dy)
        if i == 0:
            vbuf[pl.ds(my_slots, 2)] = ubuf[q]
        else:
            cp = rcopy(ubuf.at[yy], vbuf.at[pl.ds(my_slots, 2)], u_send.at[i - 1], u_recv.at[i - 1], dev(z, xx, c, yy))
            cp.start()
            usends.append(cp)
    keep_root = share(root, roots_ref, r_send, r_recv, loc.at[3])
    for i, (dx, dy) in enumerate([(0, 0), *reversed(shifts)]):
        xx, yy = lax.rem(x + XS - dx, XS), lax.rem(q + YS - dy, YS)
        ref = vbuf.at[pl.ds((xx * CORES + c) * CAP + 2 * yy, 2)]
        if i == 0:
            src = ubuf.at[q]
        else:
            src = ref
            rcopy(ref, ref, u_send.at[0], u_recv.at[len(shifts) - i], other).wait_recv()
        cp = rcopy(src, ref, e_send.at[i], e_recv.at[i], other)
        cp.start()
        usends.append(cp)
    for i, (dx, dy) in enumerate([(0, 0), *reversed(shifts)]):
        xx, yy = lax.rem(x + XS - dx, XS), lax.rem(q + YS - dy, YS)
        ref = vbuf.at[pl.ds((xx * CORES + 1 - c) * CAP + 2 * yy, 2)]
        rcopy(ref, ref, e_send.at[i], e_recv.at[i], other).wait_recv()

    def chosen(d, i):
        b = ((zoff(d) * XS + x) * CORES + c) * 2 + i
        return vbuf[tabs[2 + lax.div(b, N), lax.rem(b, N)]]

    wsends = []

    def zsend(src, dst, k, d):
        cp = rcopy(src, dst, w_send.at[k], w_recv.at[k], along(d))
        cp.start()
        wsends.append(cp)

    for s, sgn in enumerate((1, -1)):
        wbuf[4 + s, 0] = chosen(8, s)
        zsend(wbuf.at[4 + s, 0], bfar.at[s, 3, 0], s * 4 + 3, sgn * NEAR)
        for k in range(NEAR - 1, 0, -1):
            for i in range(2):
                wbuf[6 + s * 3 + k - 1, i] = chosen(sgn * (NEAR + k), i)
            zsend(wbuf.at[6 + s * 3 + k - 1], bfar.at[s, k - 1], s * 4 + k - 1, sgn * k)
    for k in range(NEAR - 1, 0, -1):
        for s, sgn in enumerate((1, -1)):
            for i in range(2):
                wbuf[12 + s * 3 + k - 1, i] = chosen(sgn * k, i)
            zsend(wbuf.at[12 + s * 3 + k - 1], abuf.at[s, k - 1], 8 + s * 4 + k - 1, sgn * k)
    for s, sgn in enumerate((1, -1)):
        total = [chosen(sgn * NEAR, i) for i in range(2)]
        for k in range(1, NEAR + 1):
            ref = bfar.at[s, k - 1] if k < NEAR else bfar.at[s, 3, 0]
            rcopy(ref, ref, w_send.at[0], w_recv.at[s * 4 + k - 1], other).wait_recv()
            for i in range(2):
                if k < NEAR:
                    total[i] = total[i] + bfar[s, k - 1, i]
                elif i == s:
                    total[i] = total[i] + bfar[s, 3, 0]
        for i in range(2):
            mfar[s, i] = total[i]
        zsend(mfar.at[s], abuf.at[s, 3], 8 + s * 4 + 3, sgn * NEAR)
    total = [chosen(0, i) for i in range(2)]
    for k in range(1, NEAR + 1):
        for s in range(2):
            ref = abuf.at[s, k - 1]
            rcopy(ref, ref, w_send.at[0], w_recv.at[8 + s * 4 + k - 1], other).wait_recv()
            for i in range(2):
                total[i] = total[i] + abuf[s, k - 1, i]
    for i in range(2):
        upd_ref[i] = total[i]

    for rsem, ref in ((s_recv, stats_ref), (r_recv, roots_ref)):
        for dy in range(1, YS):
            dst = ref.at[pl.ds(2 * lax.rem(q + YS - dy, YS), 2)]
            rcopy(dst, dst, s_send.at[0], rsem.at[dy - 1], other).wait_recv()
    keep_stat.wait()
    keep_root.wait()
    for cp in sends + dcopies + psends + ssends + usends + wsends:
        cp.wait_send()


def per_device(grad_blocks, owner_table, prev_stats):
    zs = lax.axis_size("dp") // (XS * CORES)
    gt = jnp.swapaxes(grad_blocks, 1, 2)
    part = N // YS
    dma = pltpu.SemaphoreType.DMA
    n_shift = XS * YS - 1
    upd, stats, roots = pl.pallas_call(
        lambda *refs: kernel(zs, *refs),
        out_shape=(
            jax.ShapeDtypeStruct((2, part, N), BF),
            jax.ShapeDtypeStruct(prev_stats.shape, F32),
            jax.ShapeDtypeStruct(prev_stats.shape, F32),
        ),
        in_specs=[
            pl.BlockSpec(memory_space=pltpu.VMEM),
            pl.BlockSpec(memory_space=pltpu.VMEM),
            pl.BlockSpec(memory_space=pl.ANY),
        ],
        out_specs=(
            pl.BlockSpec(memory_space=pltpu.VMEM),
            pl.BlockSpec(memory_space=pl.ANY),
            pl.BlockSpec(memory_space=pl.ANY),
        ),
        scratch_shapes=[
            pltpu.VMEM((2 * CORES * zs + 1, part, N), BF),
            pltpu.VMEM((n_shift, 2, part, N), BF),
            pltpu.VMEM((XS, YS, 2, part, N), BF),
            pltpu.VMEM((2, N, N), BF),
            pltpu.VMEM((2, 2, N, N), F32),
            pltpu.VMEM((2, 2, N, N), F32),
            pltpu.VMEM((2, 2, N, N), F32),
            pltpu.VMEM((4, N, N), F32),
            pltpu.VMEM((4, N, N), F32),
            pltpu.VMEM((YS, 2, part, N), BF),
            pltpu.VMEM((XS * CORES * CAP + 1, part, N), BF),
            pltpu.VMEM((18, 2, part, N), BF),
            pltpu.VMEM((2, 4, 2, part, N), BF),
            pltpu.VMEM((2, 2, part, N), BF),
            pltpu.VMEM((2, 4, 2, part, N), BF),
            pltpu.VMEM((8, N), jnp.int32),
            pltpu.SMEM((8, N), jnp.int32),
            dma((16,)), dma((17,)),
            dma((16,)), dma((16,)),
            dma((n_shift,)), dma((n_shift,)),
            dma((3,)), dma((3,)), dma((3,)), dma((3,)),
            dma((n_shift,)), dma((n_shift,)),
            dma((16,)), dma((16,)),
            dma((16,)), dma((16,)),
            dma((4,)),
        ],
        compiler_params=pltpu.CompilerParams(
            collective_id=0, has_side_effects=True, vmem_limit_bytes=32 * 1024 * 1024),
    )(gt, owner_table.reshape(2, N), prev_stats)
    return jnp.swapaxes(upd, 1, 2), stats, roots


def solution(mesh):
    return jax.shard_map(
        per_device,
        mesh=mesh,
        in_specs=(P("dp", None, "mp"), P(), P("dp", None, None, None)),
        out_specs=(P("dp", None, "mp"), P("dp", None, None, None), P("dp", None, None, None)),
        check_vma=False,
    )
```

time: 366 us -> 70.8 us (0.19)
  the two profiles are of different devices: /device:TPU:1 before, /device:TPU:25 now
where the time goes in v1:
time: 70.8 us; the launch traced here: 70.6 us
  Pallas kernels  64.7 us (91%)
  local copies, waits for them, and re-layouts  5.16 us (7%)
    pallas_call x1, Pallas kernels, per_device(): pl.pallas_call(lambda *refs: kernel(zs, *refs), out_shape=(jax.ShapeDtype...  64.7 us
    unnamed x9, local copies, waits for them, and re-layouts  5.16 us

profile of v1, /device:TPU:25, one launch (start us, length us, event | category | flops | bytes accessed | tf_op | source)
XLA Modules:
  0.0 70.6 jit_solution(4983998636104215052)
XLA Ops:
  0.6 0.0 copy-start.2
  0.6 0.7 copy-done.2
  1.3 0.0 copy-start
  1.3 1.2 %copy-done = f32[8,2,128,128]{3,2,1,0:T(8,128)S(1)} copy-done((f32[8,2,128,128]{3,2,1,0:T(8,128)S(1)}, f32[8,2,128,128]{3,2,1,0:T(8,128)}, u32[]{:S(2)}) %copy-start) | copy-done | bytes 1048600
  2.5 0.0 copy-start.1
  2.5 0.7 %copy-done.1 = bf16[2,128,32]{1,2,0:T(8,128)(2,1)S(1)} copy-done((bf16[2,128,32]{1,2,0:T(8,128)(2,1)S(1)}, bf16[2,128,32]{1,2,0:T(8,128)(2,1)}, u32[]{:S(2)}) %copy-start.1) | copy-done | bytes 16408
  3.3 64.7 %shard_map.58 = (bf16[2,32,128]{2,1,0:T(8,128)(2,1)S(1)}, f32[8,2,128,128]{3,2,1,0:T(8,128)S(1)}, f32[8,2,128,128]{3,2,1,0:T(8,128)S(1)}) custom-call(bf16[2,32,128]{2,1,0:T(8,128)(2,1)S(1)} %bitcast.3, s32[2,128]{1,0:T(2,128)S(1)} %bitcast.5, f32[8,2,128,128]{3,2,1,0:T(8,128)S(1)} %copy-done), custom_call_target="tpu_custom_call" | custom-call | tf_op jit(solution)/shard_map/pallas_call | solution.py:353
  68.0 0.6 copy.9
  68.6 1.0 %copy.10 = f32[8,2,128,128]{3,2,1,0:T(8,128)} copy(f32[8,2,128,128]{3,2,1,0:T(8,128)S(1)} %get-tuple-element.13) | data formatting | bytes 2097152
  69.6 1.0 %copy.11 = f32[8,2,128,128]{3,2,1,0:T(8,128)} copy(f32[8,2,128,128]{3,2,1,0:T(8,128)S(1)} %get-tuple-element.14) | data formatting | bytes 2097152
Async XLA Ops:
  0.6 0.7 copy-start.2
  1.3 1.2 %copy-start = (f32[8,2,128,128]{3,2,1,0:T(8,128)S(1)}, f32[8,2,128,128]{3,2,1,0:T(8,128)}, u32[]{:S(2)}) copy-start(f32[8,2,128,128]{3,2,1,0:T(8,128)} %refs_2_.1) | copy-start | bytes 3145732
  2.5 0.7 %copy-start.1 = (bf16[2,128,32]{1,2,0:T(8,128)(2,1)S(1)}, bf16[2,128,32]{1,2,0:T(8,128)(2,1)}, u32[]{:S(2)}) copy-start(bf16[2,128,32]{1,2,0:T(8,128)(2,1)} %param.3) | copy-start | bytes 49156

commit v2 on v1

--- a/solution.py
+++ b/solution.py
@@ -38,9 +38,9 @@
 
 def kernel(
     zs,
-    grad_ref, owner_ref, prev_ref,
+    grad_hbm, owner_hbm, prev_ref,
     upd_ref, stats_ref, roots_ref,
-    zbuf, sel1, rbuf, gt, prev, stat, root, mstate, xstate, ubuf, vbuf, wbuf, bfar, mfar, abuf, tabv, tabs,
+    zbuf, sel1, rbuf, gt, prev, stat, root, mstate, xstate, ubuf, vbuf, wbuf, bfar, mfar, abuf, tabv, tabs, grad_ref, owner_ref,
     z_send, z_recv, d_send, d_recv, p_send, p_recv, s_send, s_recv, r_send, r_recv,
     u_send, u_recv, e_send, e_recv, w_send, w_recv, loc,
 ):
@@ -50,6 +50,11 @@
     x = lax.rem(lax.div(dp, CORES), XS)
     c = lax.rem(dp, CORES)
 
+    load_owner = pltpu.make_async_copy(owner_hbm, owner_ref, loc.at[1])
+    load_owner.start()
+    load_grad = pltpu.make_async_copy(grad_hbm, grad_ref, loc.at[2])
+    load_grad.start()
+
     def zoff(d):
         return lax.rem(z + (d + zs), zs)
 
@@ -84,6 +89,7 @@
     load_prev = pltpu.make_async_copy(prev_ref.at[pl.ds(2 * q, 2)], prev, loc.at[0])
     load_prev.start()
 
+    load_owner.wait()
     owners = owner_ref[...]
     lanes = lax.broadcasted_iota(jnp.int32, (N, N), 1)
     subs = lax.broadcasted_iota(jnp.int32, (N, N), 0)
@@ -118,6 +124,7 @@
     zbuf[none_slot] = zeros
     vbuf[n_plane] = zeros
 
+    load_grad.wait()
     pl.semaphore_wait(barrier, len(partners))
 
     def zplace(cc, zz):
@@ -358,14 +365,14 @@
             jax.ShapeDtypeStruct(prev_stats.shape, F32),
         ),
         in_specs=[
-            pl.BlockSpec(memory_space=pltpu.VMEM),
-            pl.BlockSpec(memory_space=pltpu.VMEM),
-            pl.BlockSpec(memory_space=pl.ANY),
+            pl.BlockSpec(memory_space=pltpu.HBM),
+            pl.BlockSpec(memory_space=pltpu.HBM),
+            pl.BlockSpec(memory_space=pltpu.HBM),
         ],
         out_specs=(
             pl.BlockSpec(memory_space=pltpu.VMEM),
-            pl.BlockSpec(memory_space=pl.ANY),
-            pl.BlockSpec(memory_space=pl.ANY),
+            pl.BlockSpec(memory_space=pltpu.VMEM),
+            pl.BlockSpec(memory_space=pltpu.VMEM),
         ),
         scratch_shapes=[
             pltpu.VMEM((2 * CORES * zs + 1, part, N), BF),
@@ -385,6 +392,8 @@
             pltpu.VMEM((2, 4, 2, part, N), BF),
             pltpu.VMEM((8, N), jnp.int32),
             pltpu.SMEM((8, N), jnp.int32),
+            pltpu.VMEM((2, part, N), BF),
+            pltpu.VMEM((2, N), jnp.int32),
             dma((16,)), dma((17,)),
             dma((16,)), dma((16,)),
             dma((n_shift,)), dma((n_shift,)),
@@ -395,9 +404,30 @@
             dma((4,)),
         ],
         compiler_params=pltpu.CompilerParams(
-            collective_id=0, has_side_effects=True, vmem_limit_bytes=32 * 1024 * 1024),
-    )(gt, owner_table.reshape(2, N), prev_stats)
+            collective_id=0, has_side_effects=True, vmem_limit_bytes=40 * 1024 * 1024),
+    )(*[pltpu.with_memory_space_constraint(a, pltpu.HBM) for a in (gt, owner_table.reshape(2, N), prev_stats)])
+    upd, stats, roots = write_out(upd, stats, roots)
     return jnp.swapaxes(upd, 1, 2), stats, roots
+
+
+def write_kernel(*refs):
+    ins, outs, sems = refs[:3], refs[3:6], refs[6]
+    copies = [pltpu.make_async_copy(ins[k], outs[k], sems.at[k]) for k in range(3)]
+    for cp in copies:
+        cp.start()
+    for cp in copies:
+        cp.wait()
+
+
+def write_out(*arrays):
+    return pl.pallas_call(
+        write_kernel,
+        out_shape=tuple(jax.ShapeDtypeStruct(a.shape, a.dtype) for a in arrays),
+        in_specs=[pl.BlockSpec(memory_space=pltpu.VMEM)] * 3,
+        out_specs=(pl.BlockSpec(memory_space=pltpu.HBM),) * 3,
+        scratch_shapes=[pltpu.SemaphoreType.DMA((3,))],
+        compiler_params=pltpu.CompilerParams(vmem_limit_bytes=16 * 1024 * 1024),
+    )(*arrays)
 
 
 def solution(mesh):

time: 70.8 us -> 65.4 us (0.924)
  the two profiles are of different devices: /device:TPU:25 before, /device:TPU:1 now
where the time goes in v2:
time: 65.4 us; the launch traced here: 65 us
  Pallas kernels  64.3 us (98%)
    pallas_call x1, Pallas kernels, per_device(): pl.pallas_call(lambda *refs: kernel(zs, *refs), out_shape=(jax.ShapeDtype...  63 us
    pallas_call x1, Pallas kernels, write_out(): pl.pallas_call(write_kernel, out_shape=tuple((jax.ShapeDtypeStruct(a.shap...  1.35 us

profile of v2, /device:TPU:1, one launch (start us, length us, event | category | flops | bytes accessed | tf_op | source)
XLA Modules:
  0.0 65.0 jit_solution(15168244808521078095)
XLA Ops:
  0.6 63.0 %shard_map.58 = (bf16[2,32,128]{2,1,0:T(8,128)(2,1)S(1)}, f32[8,2,128,128]{3,2,1,0:T(8,128)S(1)}, f32[8,2,128,128]{3,2,1,0:T(8,128)S(1)}) custom-call(bf16[2,32,128]{2,1,0:T(8,128)(2,1)} %bitcast.3, s32[2,128]{1,0:T(2,128)} %bitcast.4, f32[8,2,128,128]{3,2,1,0:T(8,128)} %refs_2_.1), custom_call_target="tpu_custom_call" | custom-call | tf_op jit(solution)/shard_map/pallas_call | solution.py:360
  63.6 1.3 %shard_map.59 = (bf16[2,32,128]{2,1,0:T(8,128)(2,1)}, f32[8,2,128,128]{3,2,1,0:T(8,128)}, f32[8,2,128,128]{3,2,1,0:T(8,128)}) custom-call(bf16[2,32,128]{2,1,0:T(8,128)(2,1)S(1)} %get-tuple-element.9.refs_0_, f32[8,2,128,128]{3,2,1,0:T(8,128)S(1)} %get-tuple-element.10.refs_1_, f32[8,2,128,128]{3,2,1,0:T(8,128)S(1)} %get-tuple-element.11.refs_2_), custom_call_target="tpu_custom_call" | custom-call | tf_op jit(solution)/shard_map/pallas_call | solution.py:423
